TPU v7x, 256 devices: a whole 4x4x8 slice. The times are simulated.
256 devices in a mesh: samp: 8 (over x, core), snp: 32 (over y, z).
Axes of the slice: x: 4, y: 4, z: 8, core: 2. Of those that a mesh axis runs over, the one named last changes fastest.
Arguments:
- genotype: bfloat16 [40960, 40960], P('samp', 'snp'), may hold values from 0 to 2, as said below
- centre: float32 [40960], P('snp'), may hold values from 0.1 to 1
- spread: float32 [40960], P('snp'), may hold values from 0.308 to 0.7072
- pheno_probes: float32 [32, 40960], P(None, ('samp', 'snp')), may hold values from -15.75 to 15.75
Outputs:
- solution: float32 [32, 40960], P(None, ('samp', 'snp'))
- marker_stats: float32 [32, 40960], P(None, 'snp')
Inputs may be any that keep to these rules, and one draw needn't show every extreme that they name: `genotype`: whole numbers.
All inputs are finite; a program needn't handle non-finite values.
Results may differ from a plain program's by a relative error of at most 0.0003.
Values sent between devices are 32-bit elements; how exact they have to be, the bound alone decides.
A program may use at most 128 MiB of HBM per device.

v0:
```python
import math

import jax
import jax.numpy as jnp
from jax import lax
from jax.sharding import PartitionSpec as P

SAMPLES = 40960
MARKERS = 40960
ROUNDS = 3


ridge = 0.1
exact = lax.Precision.HIGHEST


def sent_to_all(array, axis):
    copies = jnp.broadcast_to(array, (lax.axis_size(axis), *array.shape))
    return lax.all_to_all(copies, axis, split_axis=0, concat_axis=0, tiled=True)


def of_everyone(array, axis):
    everything = sent_to_all(array, axis)
    return jnp.sum(everything, axis=0)


def padded_to(lines, peers):
    spare = -lines.shape[0] % peers
    if not spare:
        return lines
    return jnp.concatenate([lines, jnp.zeros((spare, *lines.shape[1:]), lines.dtype)])


def in_order(tiles, dim):
    tiles = jnp.moveaxis(tiles, 0, dim)
    dims = tiles.shape
    return tiles.reshape(*dims[:dim], dims[dim] * dims[dim + 1], *dims[dim + 2 :])


def collect(array, axis, dim):
    return in_order(sent_to_all(array, axis), dim)


def cut_along(array, dim, peers):
    before, after = (array.shape[:dim], array.shape[dim + 1 :])
    return jnp.moveaxis(array.reshape(*before, peers, -1, *after), dim, 0)


def sum_at_owner(array, axis, dim):
    tiles = cut_along(array, dim, lax.axis_size(axis))
    arrived = lax.all_to_all(tiles, axis, split_axis=0, concat_axis=0, tiled=True)
    return arrived.sum(axis=0)


def sum_by_parts(array, axes):
    lines = array.reshape(-1, array.shape[-1])
    padded = padded_to(lines, lax.axis_size(axes))
    whole = collect(sum_at_owner(padded, axes, 0), axes, 0)
    return lax.slice_in_dim(whole, 0, len(lines)).reshape(array.shape)


def local(genotype, centre, spread, pheno_probes):
    scores = (genotype.astype(jnp.float32) - centre[None, :]) / spread[None, :]
    trait_vectors = pheno_probes.shape[0]
    shard_rows = pheno_probes.shape[1]
    marker_cols = scores.shape[1]

    def marker_loads(vector):
        partial_loads = jnp.dot(vector, scores, precision=exact, preferred_element_type=jnp.float32)
        return of_everyone(partial_loads, "samp")

    def operate(vector):
        marker_load = marker_loads(vector)
        partial_image = lax.dot_general(
            marker_load,
            scores,
            (((1,), (1,)), ((), ())),
            precision=exact,
            preferred_element_type=jnp.float32,
        )
        summed = sum_by_parts(partial_image, "snp")
        return (summed / MARKERS + ridge * vector, marker_load)

    def column_totals_vector(increment_terms):
        local_partial_sums = tuple(
            (jnp.sum(increment_term, axis=1, keepdims=True) for increment_term in increment_terms)
        )
        totals = jax.tree.map(lambda part: of_everyone(part, "samp"), local_partial_sums)
        return totals

    right_side = collect(pheno_probes, "snp", 1)
    solution = jnp.zeros_like(right_side)
    stats_total = jnp.zeros((trait_vectors, marker_cols), jnp.float32)
    applied, marker_load = operate(right_side)
    norm_start, coupled = column_totals_vector((right_side * right_side, right_side * applied))
    step_start = norm_start / coupled

    def combined_update(counter, carried):
        solution, residual, direction, applied_dir, dir_loads, stats_total, norm_now, step_size = (
            carried
        )
        solution = solution + step_size * direction
        stats_total = stats_total + step_size * dir_loads
        residual = residual - step_size * applied_dir
        applied, marker_load = operate(residual)
        norm_next, coupled = column_totals_vector((residual * residual, residual * applied))
        previous_quotient = norm_next / norm_now
        step_next = norm_next / (coupled - previous_quotient * norm_next / step_size)
        direction = residual + previous_quotient * direction
        applied_dir = applied + previous_quotient * applied_dir
        dir_loads = marker_load + previous_quotient * dir_loads
        return (
            solution,
            residual,
            direction,
            applied_dir,
            dir_loads,
            stats_total,
            norm_next,
            step_next,
        )

    carried = (
        solution,
        right_side,
        right_side,
        applied,
        marker_load,
        stats_total,
        norm_start,
        step_start,
    )
    carried = lax.fori_loop(0, ROUNDS - 1, combined_update, carried)
    solution, residual, direction, applied_dir, dir_loads, stats_total, norm_now, step_size = (
        carried
    )
    solution = solution + step_size * direction
    stats_total = stats_total + step_size * dir_loads
    marker_stats = stats_total / math.sqrt(SAMPLES)
    own_solution = lax.dynamic_slice_in_dim(
        solution, lax.axis_index("snp") * shard_rows, shard_rows, 1
    )
    return (own_solution, marker_stats)


def solution(mesh):
    in_specs = (P("samp", "snp"), P("snp"), P("snp"), P(None, ("samp", "snp")))
    out_specs = (P(None, ("samp", "snp")), P(None, "snp"))
    return jax.shard_map(local, mesh=mesh, in_specs=in_specs, out_specs=out_specs, check_vma=False)
```

profile of v0, /device:TPU:1, one launch (start us, length us, event | category | flops | bytes accessed | tf_op | source)
XLA Modules:
  0.0 462.5 jit_solution(10409636832691590941)
XLA Ops:
  0.6 1.8 broadcast_in_dim.40
  2.5 12.0 %all-to-all-start.5 = ((f32[32,32,160]{2,1,0:T(8,128)}), f32[32,32,160]{2,1,0:T(8,128)S(1)}, u32[]{:S(2)}, u32[]{:S(2)}) async-start(f32[32,32,160]{2,1,0:T(8,128)} %broadcast_in_dim.40), calls=%async_computation.5 | async-start | bytes 2097152 | tf_op jit(solution)/shard_map/all_to_all | solution.py:19
  14.5 14.8 %subtract_divide_fusion = f32[5120,1280]{1,0:T(8,128)} fusion(bf16[5120,1280]{1,0:T(8,128)(2,1)} %param.6, f32[1280]{0:T(1024)} %param.8, f32[1280]{0:T(1024)} %param.7), kind=kLoop, calls=%fused_computation.13 | loop fusion | flops 19660800 | bytes 39331840 | tf_op jit(solution)/shard_map/div | solution.py:63
  29.3 10.1 %all-to-all-done.5 = f32[32,32,160]{2,1,0:T(8,128)S(1)} async-done(((f32[32,32,160]{2,1,0:T(8,128)}), f32[32,32,160]{2,1,0:T(8,128)S(1)}, u32[]{:S(2)}, u32[]{:S(2)}) %all-to-all-start.5) | async-done | bytes 655392 | tf_op jit(solution)/shard_map/all_to_all | solution.py:19
  39.4 0.6 copy.30
  40.0 0.6 reshape.46
  40.6 18.8 %convolution_bitcast_fusion.2 = f32[32,1280]{1,0:T(8,128)S(1)} fusion(f32[5120,1280]{1,0:T(8,128)} %subtract_divide_fusion, f32[32,5120]{1,0:T(8,128)S(1)} %reshape.46), kind=kOutput, calls=%fused_computation.15 | convolution fusion | flops 2516582400 | bytes 27033600 | tf_op jit(solution)/shard_map/dot_general | solution.py:69
  59.5 0.1 broadcast_in_dim.41
  59.6 26.5 %all_to_all.65 = f32[8,32,1280]{2,1,0:T(8,128)S(1)} all-to-all(f32[8,32,1280]{2,1,0:T(8,128)S(1)} %broadcast_in_dim.41), channel_id=1, replica_groups=mesh['samp'=8,'snp'=32] {'samp'}, dimensions={0} | all-to-all | bytes 2621440 | tf_op jit(solution)/shard_map/all_to_all | solution.py:19
  86.2 26.6 %convolution_bitcast_fusion.1 = f32[32,1,5120]{2,0,1:T(8,128)S(1)} fusion(f32[32,1280]{1,0:T(8,128)S(1)} %reduce_sum.116, f32[5120,1280]{1,0:T(8,128)} %subtract_divide_fusion), kind=kOutput, calls=%fused_computation.14 | convolution fusion | flops 2516582400 | bytes 27033600 | tf_op jit(solution)/shard_map/dot_general | solution.py:74
  112.8 0.7 copy.14
  113.5 21.5 %all_to_all.66 = f32[32,1,5120]{2,1,0:T(1,128)S(1)} all-to-all(f32[32,1,5120]{2,1,0:T(1,128)S(1)} %copy.14), channel_id=1, replica_groups=mesh['samp'=8,'snp'=32] {'snp'}, dimensions={0} | all-to-all | bytes 1310720 | tf_op jit(solution)/shard_map/all_to_all | solution.py:51
  134.9 0.4 reduce_sum.117
  135.3 0.3 broadcast_in_dim.42
  135.6 24.3 %all_to_all.67 = f32[32,1,5120]{2,1,0:T(1,128)S(1)} all-to-all(f32[32,1,5120]{2,1,0:T(1,128)S(1)} %broadcast_in_dim.42), channel_id=1, replica_groups=mesh['samp'=8,'snp'=32] {'snp'}, dimensions={0} | all-to-all | bytes 1310720 | tf_op jit(solution)/shard_map/all_to_all | solution.py:19
  160.0 0.1 copy_multiply_fusion
  160.1 1.6 div.50
  161.7 2.1 multiply_reduce_fusion.2
  163.7 0.6 broadcast_in_dim.44
  164.3 7.8 %all-to-all-start.9 = ((f32[8,32,1]{1,2,0:T(1,128)}), f32[8,32,1]{1,2,0:T(1,128)S(1)}, u32[]{:S(2)}, u32[]{:S(2)}) async-start(f32[8,32,1]{1,2,0:T(1,128)} %broadcast_in_dim.44), calls=%async_computation.9 | async-start | bytes 8192 | tf_op jit(solution)/shard_map/all_to_all | solution.py:19
  172.2 4.5 all-to-all-done.9
  176.7 0.6 broadcast_in_dim.45
  177.3 3.9 all-to-all-start.10
  181.2 0.2 bitcast_add_fusion.1
  181.4 4.3 all-to-all-done.10
  185.7 273.5 %while.25 = (s32[]{:T(128)}, f32[32,5120]{1,0:T(8,128)}, f32[32,5120]{1,0:T(8,128)S(1)}, f32[32,5120]{1,0:T(8,128)S(1)}, f32[32,5120]{1,0:T(8,128)S(1)}, /*index...) while((s32[]{:T(128)}, f32[32,5120]{1,0:T(8,128)}, ...), condition=%wide.region_13.0_spmd.clone, body=%wide.region_6.0_spmd.clone.sunk | while | flops 5036764160 | bytes 80832344 | solution.py:133
  185.8 0.2 multiply_subtract_fusion.2
  186.0 17.7 %fusion.20 = f32[32,1280]{1,0:T(8,128)S(1)} fusion(f32[32,5120]{1,0:T(8,128)S(1)} %multiply_subtract_fusion.2, f32[5120,1280]{1,0:T(8,128)} %get-tuple-element.241), kind=kOutput, calls=%fused_computation.25.clone.1 | convolution fusion | flops 2516582400 | bytes 27033600 | tf_op jit(solution)/shard_map/while/body/eval_jaxpr/dot_general | solution.py:69
  203.7 0.1 broadcast_in_dim.54
  203.8 20.9 %all_to_all.68 = f32[8,32,1280]{2,1,0:T(8,128)S(1)} all-to-all(f32[8,32,1280]{2,1,0:T(8,128)S(1)} %broadcast_in_dim.54), channel_id=1, replica_groups=mesh['samp'=8,'snp'=32] {'samp'}, dimensions={0} | all-to-all | bytes 2621440 | tf_op jit(solution)/shard_map/while/body/eval_jaxpr/all_to_all | solution.py:19
  224.7 26.6 %convolution_bitcast_fusion.4 = f32[32,1,5120]{2,0,1:T(8,128)S(1)} fusion(f32[32,1280]{1,0:T(8,128)S(1)} %reduce_sum.142, f32[5120,1280]{1,0:T(8,128)} %get-tuple-element.241), kind=kOutput, calls=%fused_computation.clone.1 | convolution fusion | flops 2516582400 | bytes 27033600 | tf_op jit(solution)/shard_map/while/body/eval_jaxpr/dot_general | solution.py:74
  251.3 0.7 copy.36
  252.0 21.2 %all_to_all.69 = f32[32,1,5120]{2,1,0:T(1,128)S(1)} all-to-all(f32[32,1,5120]{2,1,0:T(1,128)S(1)} %copy.36), channel_id=1, replica_groups=mesh['samp'=8,'snp'=32] {'snp'}, dimensions={0} | all-to-all | bytes 1310720 | tf_op jit(solution)/shard_map/while/body/eval_jaxpr/all_to_all | solution.py:51
  273.2 0.4 reduce_sum.143
  273.6 0.3 broadcast_in_dim.55
  273.9 24.3 %all_to_all.70 = f32[32,1,5120]{2,1,0:T(1,128)S(1)} all-to-all(f32[32,1,5120]{2,1,0:T(1,128)S(1)} %broadcast_in_dim.55), channel_id=1, replica_groups=mesh['samp'=8,'snp'=32] {'snp'}, dimensions={0} | all-to-all | bytes 1310720 | tf_op jit(solution)/shard_map/while/body/eval_jaxpr/all_to_all | solution.py:19
  298.2 0.7 broadcast_multiply_fusion.2
  298.9 0.3 multiply_reduce_fusion.5
  299.2 11.6 %all_to_all.71 = f32[8,32,1]{1,2,0:T(1,128)S(1)} all-to-all(f32[8,32,1]{1,2,0:T(1,128)S(1)} %broadcast_in_dim.57), channel_id=1, replica_groups=mesh['samp'=8,'snp'=32] {'samp'}, dimensions={0} | all-to-all | bytes 2048 | tf_op jit(solution)/shard_map/while/body/eval_jaxpr/all_to_all | solution.py:19
  310.8 0.6 broadcast_in_dim.56
  311.4 3.9 all-to-all-start.3
  315.3 4.5 all-to-all-done.3
  319.9 0.6 multiply_add_fusion.4
  320.5 2.0 select_add_fusion.3
  322.4 0.2 multiply_subtract_fusion.2
  322.7 17.7 %fusion.20 = f32[32,1280]{1,0:T(8,128)S(1)} fusion(f32[32,5120]{1,0:T(8,128)S(1)} %multiply_subtract_fusion.2, f32[5120,1280]{1,0:T(8,128)} %get-tuple-element.241), kind=kOutput, calls=%fused_computation.25.clone.1 | convolution fusion | flops 2516582400 | bytes 27033600 | tf_op jit(solution)/shard_map/while/body/eval_jaxpr/dot_general | solution.py:69
  340.4 0.1 broadcast_in_dim.54
  340.5 20.9 %all_to_all.68 = f32[8,32,1280]{2,1,0:T(8,128)S(1)} all-to-all(f32[8,32,1280]{2,1,0:T(8,128)S(1)} %broadcast_in_dim.54), channel_id=1, replica_groups=mesh['samp'=8,'snp'=32] {'samp'}, dimensions={0} | all-to-all | bytes 2621440 | tf_op jit(solution)/shard_map/while/body/eval_jaxpr/all_to_all | solution.py:19
  361.4 26.6 %convolution_bitcast_fusion.4 = f32[32,1,5120]{2,0,1:T(8,128)S(1)} fusion(f32[32,1280]{1,0:T(8,128)S(1)} %reduce_sum.142, f32[5120,1280]{1,0:T(8,128)} %get-tuple-element.241), kind=kOutput, calls=%fused_computation.clone.1 | convolution fusion | flops 2516582400 | bytes 27033600 | tf_op jit(solution)/shard_map/while/body/eval_jaxpr/dot_general | solution.py:74
  388.0 0.7 copy.36
  388.7 21.2 %all_to_all.69 = f32[32,1,5120]{2,1,0:T(1,128)S(1)} all-to-all(f32[32,1,5120]{2,1,0:T(1,128)S(1)} %copy.36), channel_id=1, replica_groups=mesh['samp'=8,'snp'=32] {'snp'}, dimensions={0} | all-to-all | bytes 1310720 | tf_op jit(solution)/shard_map/while/body/eval_jaxpr/all_to_all | solution.py:51
  409.9 0.4 reduce_sum.143
  410.2 0.3 broadcast_in_dim.55
  410.6 24.3 %all_to_all.70 = f32[32,1,5120]{2,1,0:T(1,128)S(1)} all-to-all(f32[32,1,5120]{2,1,0:T(1,128)S(1)} %broadcast_in_dim.55), channel_id=1, replica_groups=mesh['samp'=8,'snp'=32] {'snp'}, dimensions={0} | all-to-all | bytes 1310720 | tf_op jit(solution)/shard_map/while/body/eval_jaxpr/all_to_all | solution.py:19
  434.9 0.7 broadcast_multiply_fusion.2
  435.6 0.3 multiply_reduce_fusion.5
  435.9 11.6 %all_to_all.71 = f32[8,32,1]{1,2,0:T(1,128)S(1)} all-to-all(f32[8,32,1]{1,2,0:T(1,128)S(1)} %broadcast_in_dim.57), channel_id=1, replica_groups=mesh['samp'=8,'snp'=32] {'samp'}, dimensions={0} | all-to-all | bytes 2048 | tf_op jit(solution)/shard_map/while/body/eval_jaxpr/all_to_all | solution.py:19
  447.4 0.6 broadcast_in_dim.56
  448.0 3.9 all-to-all-start.3
  452.0 4.5 all-to-all-done.3
  456.5 0.6 multiply_add_fusion.4
  457.1 2.1 select_add_fusion.3
  459.2 1.7 add_multiply_fusion
  461.0 1.5 dynamic-slice_add_fusion
  (31 shorter events, 0.5 us)
Async XLA Ops:
  2.5 36.9 %all-to-all-start.5 = ((f32[32,32,160]{2,1,0:T(8,128)}), f32[32,32,160]{2,1,0:T(8,128)S(1)}, u32[]{:S(2)}, u32[]{:S(2)}) async-start(f32[32,32,160]{2,1,0:T(8,128)} %broadcast_in_dim.40), calls=%async_computation.5 | async-start | bytes 2097152 | tf_op jit(solution)/shard_map/all_to_all | solution.py:19
  86.2 85.9 %copy-start.2 = (f32[32,1280]{1,0:T(8,128)}, f32[32,1280]{1,0:T(8,128)S(1)}, u32[]{:S(2)}) copy-start(f32[32,1280]{1,0:T(8,128)S(1)} %reduce_sum.116) | copy-start | bytes 491524
  164.3 12.3 %all-to-all-start.9 = ((f32[8,32,1]{1,2,0:T(1,128)}), f32[8,32,1]{1,2,0:T(1,128)S(1)}, u32[]{:S(2)}, u32[]{:S(2)}) async-start(f32[8,32,1]{1,2,0:T(1,128)} %broadcast_in_dim.44), calls=%async_computation.9 | async-start | bytes 8192 | tf_op jit(solution)/shard_map/all_to_all | solution.py:19
  177.3 8.5 %all-to-all-start.10 = ((f32[8,32,1]{1,2,0:T(1,128)}), f32[8,32,1]{1,2,0:T(1,128)S(1)}, u32[]{:S(2)}, u32[]{:S(2)}) async-start(f32[8,32,1]{1,2,0:T(1,128)} %broadcast_in_dim.45), calls=%async_computation.10 | async-start | bytes 8192 | tf_op jit(solution)/shard_map/all_to_all | solution.py:19
  224.7 95.1 %copy-start = (f32[32,5120]{1,0:T(8,128)S(1)}, f32[32,5120]{1,0:T(8,128)}, u32[]{:S(2)}) copy-start(f32[32,5120]{1,0:T(8,128)} %get-tuple-element.220) | copy-start | bytes 1966084 | tf_op jit(solution)/shard_map/while
  311.4 8.5 %all-to-all-start.3 = ((f32[8,32,1]{1,2,0:T(1,128)}), f32[8,32,1]{1,2,0:T(1,128)S(1)}, u32[]{:S(2)}, u32[]{:S(2)}) async-start(f32[8,32,1]{1,2,0:T(1,128)} %broadcast_in_dim.56), calls=%async_computation.3 | async-start | bytes 8192 | tf_op jit(solution)/shard_map/while/body/eval_jaxpr/all_to_all | solution.py:19
  320.5 2.0 copy-start.1
  361.4 95.1 %copy-start = (f32[32,5120]{1,0:T(8,128)S(1)}, f32[32,5120]{1,0:T(8,128)}, u32[]{:S(2)}) copy-start(f32[32,5120]{1,0:T(8,128)} %get-tuple-element.220) | copy-start | bytes 1966084 | tf_op jit(solution)/shard_map/while
  448.0 8.5 %all-to-all-start.3 = ((f32[8,32,1]{1,2,0:T(1,128)}), f32[8,32,1]{1,2,0:T(1,128)S(1)}, u32[]{:S(2)}, u32[]{:S(2)}) async-start(f32[8,32,1]{1,2,0:T(1,128)} %broadcast_in_dim.56), calls=%async_computation.3 | async-start | bytes 8192 | tf_op jit(solution)/shard_map/while/body/eval_jaxpr/all_to_all | solution.py:19
  457.1 2.1 copy-start.1
where the time goes:
time: 464 us; the launch traced here: 462 us
  blocking collectives  228 us (49%)
  matrix products  134 us (29%)
  starting transfers between devices  31.5 us (7%)
  other arithmetic  29.5 us (6%)
  waiting for transfers between devices  28 us (6%)
  local copies, waits for them, and re-layouts  10.5 us (2%)
    all_to_all x8, blocking collectives, sent_to_all(): return lax.all_to_all(copies, axis, split_axis=0, concat_axis=0, tiled=True)  164 us
    dot_general x3, matrix products, operate(): lax.dot_general(marker_load, scores, (((1,), (1,)), ((), ())), precision=...  79.7 us
    all_to_all x3, blocking collectives, sum_at_owner(): lax.all_to_all(tiles, axis, split_axis=0, concat_axis=0, tiled=True)  63.8 us
    dot_general x3, matrix products, marker_loads(): jnp.dot(vector, scores, precision=exact, preferred_element_type=jnp.float32)  54.2 us
    all_to_all x5, starting transfers between devices, sent_to_all(): return lax.all_to_all(copies, axis, split_axis=0, concat_axis=0, tiled=True)  31.5 us
    all_to_all x5, waiting for transfers between devices, sent_to_all(): return lax.all_to_all(copies, axis, split_axis=0, concat_axis=0, tiled=True)  28 us
    div x1, other arithmetic, local(): scores = (genotype.astype(jnp.float32) - centre[None, :]) / spread[None, :]  14.8 us
  transfers between devices with their start and end apart: 5, of which 5 were waited for; matrix products, arithmetic and copies ran while one was open for 3% of the time, Pallas kernels for 0%

commit v1 on v0

v1 whole, which is shorter than its diff:
```python
import math

import jax
import jax.numpy as jnp
from jax import lax
from jax.experimental import pallas as pl
from jax.experimental.pallas import tpu as pltpu
from jax.sharding import PartitionSpec as P

SAMPLES = 40960
MARKERS = 40960
ROUNDS = 3
RIDGE = 0.1

ROWS = 32
NY, NZ = 4, 8
NX = 4
PEERS = NY * NZ
CHUNK = 640
BLOCK = CHUNK * NZ
COLS = 1280
WIDE = COLS + 128
PIECE = 8 * CHUNK

MESH = pl.DeviceIdType.MESH
NEAR = (1, 7, 2, 6, 3, 5, 4)
f32 = jnp.float32


def near(step):
    half = (step + 1) // 2
    return jnp.where(step % 2 == 1, half, (NZ - half) % NZ)


def split(value):
    high = value.astype(jnp.bfloat16)
    rest = value - high.astype(f32)
    return high, rest.astype(jnp.bfloat16)


def lanes_summed(value):
    total = value[:, 0:128]
    for tile in range(1, value.shape[1] // 128):
        total = total + value[:, 128 * tile : 128 * (tile + 1)]
    return total


def kernel(
    geno_hbm, rhs_ref, centre_ref, spread_ref, solution_ref, stats_ref,
    geno, r_0, r_1, r_2, packed, u_0, u_1, from_y_0, from_y_1, to_z_0, to_z_1,
    from_z_0, from_z_1, partial, acc, loads_out, from_core, by_x, loads_in,
    scalars, lhs, dir_loads, steps, betas,
    geno_sem, s_gz, s_gy, s_ry, s_rz, s_core, s_x, s_back, s_sc,
    gz, gy, ry, rz, core_sem, x_sem, back_sem, sc_sem,
):
    samp, snp = lax.axis_index("samp"), lax.axis_index("snp")
    x, core = samp // 2, samp % 2
    y, z = snp // NZ, snp % NZ
    residuals = (r_0, r_1, r_2)

    def at_z(other):
        return (samp, y * NZ + other)

    def at_y(other):
        return (samp, other * NZ + z)

    def at_x(other):
        return (other * 2 + core, snp)

    partner = (x * 2 + 1 - core, snp)

    def send(source, target, send_sem, recv_sem, device):
        pltpu.make_async_remote_copy(
            source, target, send_sem, recv_sem, device_id=device, device_id_type=MESH
        ).start()

    def settle(sem, like):
        pltpu.make_async_copy(like, like, sem).wait()

    pieces = r_0.at[0:24, 0:CHUNK]

    def rows_of(group):
        return pl.ds(pl.multiple_of(group * 8, 8), 8)

    def cols_of(chunk):
        return pl.ds(pl.multiple_of(chunk * CHUNK, 128), CHUNK)

    for zz in range(NZ):
        for yy in range(NY):
            first = 160 * (yy * NZ + zz)
            pltpu.make_async_copy(
                geno_hbm.at[pl.ds(first, 128)], geno.at[pl.ds(CHUNK * zz + 128 * yy, 128)], geno_sem
            ).start()
            pltpu.make_async_copy(
                geno_hbm.at[pl.ds(first + 128, 32)],
                geno.at[pl.ds(CHUNK * zz + 512 + 32 * yy, 32)],
                geno_sem,
            ).start()

    barrier = pltpu.get_barrier_semaphore()

    def greet(offset, carry):
        pl.semaphore_signal(
            barrier, inc=1, device_id=(samp, (snp + offset) % PEERS), device_id_type=MESH
        )
        return carry

    lax.fori_loop(1, PEERS, greet, 0)
    pl.semaphore_signal(barrier, inc=1, device_id=partner, device_id_type=MESH)
    for dx in range(1, NX):
        pl.semaphore_signal(barrier, inc=1, device_id=at_x((x + dx) % NX), device_id_type=MESH)

    def main_cols(zz):
        return pl.ds(pl.multiple_of(zz * CHUNK + y * 128, 128), 128)

    r_0[:, main_cols(z)] = rhs_ref[:, 0:128]
    tails = [rhs_ref[8 * group : 8 * group + 8, 128:160] for group in range(4)]
    packed[y, z] = jnp.concatenate(tails, axis=1)
    pl.semaphore_wait(barrier, PEERS - 1 + NX)

    def forward_own(k, zz):
        for dy in range(1, NY):
            other = at_y((y + dy) % NY)
            if k == 0:
                block = r_0.at[:, main_cols(zz)]
                send(block, block, s_gy.at[0], gy.at[0, zz], other)
                send(packed.at[y, zz], packed.at[y, zz], s_gy.at[0], gy.at[0, zz], other)
            else:
                block = residuals[k].at[rows_of(y), cols_of(zz)]
                send(block, block, s_gy.at[k], gy.at[k, zz], other)

    def gather(k):
        for d in NEAR:
            other = at_z((z + d) % NZ)
            if k == 0:
                block = r_0.at[:, main_cols(z)]
                send(block, block, s_gz.at[0], gz.at[0, d - 1], other)
                send(packed.at[y, z], packed.at[y, z], s_gz.at[0], gz.at[0, d - 1], other)
            else:
                block = residuals[k].at[rows_of(y), cols_of(z)]
                send(block, block, s_gz.at[k], gz.at[k, d - 1], other)
        forward_own(k, z)
        for d in NEAR:
            settle(gz.at[k, d - 1], r_0.at[0:8, 0:CHUNK])
            forward_own(k, (z - d + NZ) % NZ)

    lane = lax.broadcasted_iota(jnp.int32, (8, 128), 1)

    def unpack(zz):
        sources = [packed[yy, zz] for yy in range(NY)]
        for group in range(4):
            tile = jnp.zeros((8, 128), f32)
            for yy in range(NY):
                shift = (32 * (yy - group)) % 128
                moved = pltpu.roll(sources[yy], shift, 1) if shift else sources[yy]
                tile = jnp.where(lane // 32 == yy, moved, tile)
            start = pl.multiple_of(zz * CHUNK + 512, 128)
            r_0[8 * group : 8 * group + 8, pl.ds(start, 128)] = tile

    def to_loads(k):
        partial[...] = jnp.zeros_like(partial)
        acc[...] = jnp.zeros_like(acc)

        def chunk(step, carry):
            zz = (z - near(step) + NZ) % NZ
            settle(gy.at[k, zz], pieces)
            if k == 0:
                unpack(zz)
            value = residuals[k][:, cols_of(zz)]
            high, low = split(value)
            partial[...] += jnp.dot(
                jnp.concatenate([high, low], axis=0),
                geno[cols_of(zz), :],
                preferred_element_type=f32,
            )
            acc[0] += lanes_summed(high.astype(f32) + low.astype(f32))
            acc[1] += lanes_summed(value * value)
            if k > 0:
                acc[2] += lanes_summed(value * residuals[k - 1][:, cols_of(zz)])
            if k > 1:
                acc[3] += lanes_summed(value * r_0[:, cols_of(zz)])
            return carry

        lax.fori_loop(0, NZ, chunk, 0)

    lane32 = lax.broadcasted_iota(jnp.int32, (ROWS, 128), 1)
    eye = lax.broadcasted_iota(jnp.int32, (ROWS, 128), 0) == lane32

    def over_samp(k):
        out, got, halves, full = loads_out.at[k], from_core.at[k], by_x.at[k], loads_in.at[k]
        total = jnp.sum(acc[0], axis=1, keepdims=True)
        raw = partial[0:ROWS] + partial[ROWS : 2 * ROWS]
        out[:, 0:COLS] = (raw - total * centre_ref[...]) / spread_ref[...]
        tile = jnp.zeros((ROWS, 128), f32)
        for which in range(1, 2 + k):
            tile = jnp.where(lane32 == which - 1, jnp.sum(acc[which], axis=1, keepdims=True), tile)
        out[:, COLS:WIDE] = tile
        mine = pl.ds(pl.multiple_of(core * 16, 16), 16)
        theirs = pl.ds(pl.multiple_of(16 - core * 16, 16), 16)
        send(out.at[theirs], got, s_core.at[k], core_sem.at[k], partner)
        settle(core_sem.at[k], got)
        halves[x] = out[mine, :] + got[...]
        for dx in (2, 1, 3):
            send(halves.at[x], halves.at[x], s_x.at[k], x_sem.at[k], at_x((x + dx) % NX))
        settle(x_sem.at[k], halves.at[0:3])
        full[mine, :] = (halves[0] + halves[1]) + (halves[2] + halves[3])
        send(full.at[mine], full.at[mine], s_back.at[k], back_sem.at[k], partner)
        settle(back_sem.at[k], full.at[mine])

    def spread_norms(k):
        loads = dir_loads[...]
        norm = jnp.sum(lanes_summed(loads * loads), axis=1, keepdims=True)
        row = jnp.sum(jnp.where(eye, norm, 0.0), axis=0, keepdims=True)
        scalars[k, snp] = row

        def one(offset, carry):
            slot = scalars.at[k, snp]
            send(slot, slot, s_sc.at[k], sc_sem.at[k], (samp, (snp + offset) % PEERS))
            return carry

        lax.fori_loop(1, PEERS, one, 0)

    def total_norms(k):
        settle(sc_sem.at[k], scalars.at[k, 0 : PEERS - 1])
        row = jnp.sum(scalars[k], axis=0)
        return jnp.sum(jnp.where(eye, row, 0.0), axis=1, keepdims=True)

    def to_image(k):
        image, from_y, to_z, from_z = (
            (u_0, from_y_0, to_z_0, from_z_0), (u_1, from_y_1, to_z_1, from_z_1)
        )[k]
        high, low = split(dir_loads[...] / spread_ref[...])
        lhs[0:ROWS] = high
        lhs[ROWS : 2 * ROWS] = low
        shift = (high.astype(f32) + low.astype(f32)) * centre_ref[...]
        shift = jnp.sum(lanes_summed(shift), axis=1, keepdims=True)

        def chunk(step, carry):
            zz = (z + near(NZ - 1 - step)) % NZ
            both = lax.dot_general(
                lhs[...], geno[cols_of(zz), :], (((1,), (1,)), ((), ())),
                preferred_element_type=f32,
            )
            image[:, cols_of(zz)] = both[0:ROWS] + both[ROWS : 2 * ROWS] - shift
            for dy in range(1, NY):
                other = (y + dy) % NY
                send(
                    image.at[rows_of(other), cols_of(zz)], from_y.at[dy - 1, :, cols_of(zz)],
                    s_ry.at[k], ry.at[k, zz], at_y(other),
                )
            return carry

        lax.fori_loop(0, NZ, chunk, 0)

        def pass_on(step, carry):
            offset = near(NZ - 1 - step)
            zz = (z + offset) % NZ
            settle(ry.at[k, zz], pieces)
            total = image[rows_of(y), cols_of(zz)]
            for dy in range(NY - 1):
                total = total + from_y[dy, :, cols_of(zz)]
            to_z[zz] = total

            @pl.when(step < NZ - 1)
            def _():
                send(to_z.at[zz], from_z.at[offset - 1], s_rz.at[k], rz.at[k], at_z(zz))

            return carry

        lax.fori_loop(0, NZ, pass_on, 0)
        settle(rz.at[k], from_z)
        total = to_z[z]
        for d in range(NZ - 1):
            total = total + from_z[d]
        return total

    norms, squares = [], []
    for k in range(ROUNDS):
        gather(k)
        if k == 0:
            settle(geno_sem, geno)
        to_loads(k)
        over_samp(k)
        loads = loads_in[k, :, 0:COLS]
        norm = loads_in[k, :, COLS : COLS + 1]
        if k == 0:
            dir_loads[...] = loads
            square = norm
        else:
            beta = norm / norms[-1]
            dir_loads[...] = loads + beta * dir_loads[...]
            cross = loads_in[k, :, COLS + 1 : COLS + 2]
            if k == 2:
                cross = cross + betas[0][:, 0:1] * loads_in[k, :, COLS + 2 : COLS + 3]
            square = norm + 2.0 * beta * cross + beta * beta * squares[-1]
            betas[k - 1] = jnp.broadcast_to(beta, (ROWS, 128))
        norms.append(norm)
        squares.append(square)
        spread_norms(k)
        if k < ROUNDS - 1:
            summed = to_image(k)
        size = norm / (total_norms(k) * (1.0 / MARKERS) + RIDGE * square)
        steps[k] = jnp.broadcast_to(size, (ROWS, 128))
        gain = size * (1.0 / math.sqrt(SAMPLES))
        if k == 0:
            stats_ref[...] = gain * dir_loads[...]
        else:
            stats_ref[...] += gain * dir_loads[...]
        if k < ROUNDS - 1:
            mine = (rows_of(y), cols_of(z))
            direction = residuals[k][mine]
            if k == 1:
                direction = direction + betas[0, rows_of(y), 0:1] * r_0[mine]
            moved = summed * (1.0 / MARKERS) + RIDGE * direction
            residuals[k + 1][mine] = residuals[k][mine] - steps[k, rows_of(y), 0:1] * moved

    def combined(columns):
        first = r_0[:, columns]
        second = r_1[:, columns] + betas[0][:, 0:1] * first
        third = r_2[:, columns] + betas[1][:, 0:1] * second
        return steps[0][:, 0:1] * first + steps[1][:, 0:1] * second + steps[2][:, 0:1] * third

    solution_ref[:, 0:128] = combined(main_cols(z))
    tail = combined(pl.ds(pl.multiple_of(z * CHUNK + 512, 128), 128))
    for yy in range(NY):

        @pl.when(y == yy)
        def _():
            solution_ref[:, 128:160] = tail[:, 32 * yy : 32 * yy + 32]

    for k in range(ROUNDS):
        settle(s_gz.at[k], from_z_0)
        settle(s_gy.at[k], r_0.at[0:24])
        settle(s_core.at[k], from_core.at[k])
        settle(s_x.at[k], by_x.at[k, 0:3])
        settle(s_back.at[k], from_core.at[k])
        settle(s_sc.at[k], scalars.at[k, 0 : PEERS - 1])
    for k in range(ROUNDS - 1):
        settle(s_ry.at[k], r_0.at[0:24])
        settle(s_rz.at[k], from_z_0)


def local(genotype, centre, spread, pheno_probes):
    block = (ROWS, BLOCK)
    dma = pltpu.SemaphoreType.DMA
    vmem = pl.BlockSpec(memory_space=pltpu.VMEM)
    return pl.pallas_call(
        kernel,
        out_shape=(
            jax.ShapeDtypeStruct((ROWS, 160), f32),
            jax.ShapeDtypeStruct((ROWS, COLS), f32),
        ),
        in_specs=[pl.BlockSpec(memory_space=pl.ANY), vmem, vmem, vmem],
        out_specs=(vmem, vmem),
        scratch_shapes=[
            pltpu.VMEM((BLOCK, COLS), jnp.bfloat16),
            pltpu.VMEM(block, f32),
            pltpu.VMEM(block, f32),
            pltpu.VMEM(block, f32),
            pltpu.VMEM((NY, NZ, 8, 128), f32),
            pltpu.VMEM(block, f32),
            pltpu.VMEM(block, f32),
            pltpu.VMEM((NY - 1, 8, BLOCK), f32),
            pltpu.VMEM((NY - 1, 8, BLOCK), f32),
            pltpu.VMEM((NZ, 8, CHUNK), f32),
            pltpu.VMEM((NZ, 8, CHUNK), f32),
            pltpu.VMEM((NZ - 1, 8, CHUNK), f32),
            pltpu.VMEM((NZ - 1, 8, CHUNK), f32),
            pltpu.VMEM((2 * ROWS, COLS), f32),
            pltpu.VMEM((4, ROWS, 128), f32),
            pltpu.VMEM((ROUNDS, ROWS, WIDE), f32),
            pltpu.VMEM((ROUNDS, 16, WIDE), f32),
            pltpu.VMEM((ROUNDS, NX, 16, WIDE), f32),
            pltpu.VMEM((ROUNDS, ROWS, WIDE), f32),
            pltpu.VMEM((ROUNDS, PEERS, 1, 128), f32),
            pltpu.VMEM((2 * ROWS, COLS), jnp.bfloat16),
            pltpu.VMEM((ROWS, COLS), f32),
            pltpu.VMEM((ROUNDS, ROWS, 128), f32),
            pltpu.VMEM((ROUNDS - 1, ROWS, 128), f32),
            dma,
            dma((ROUNDS,)),
            dma((ROUNDS,)),
            dma((ROUNDS - 1,)),
            dma((ROUNDS - 1,)),
            dma((ROUNDS,)),
            dma((ROUNDS,)),
            dma((ROUNDS,)),
            dma((ROUNDS,)),
            dma((ROUNDS, NZ - 1)),
            dma((ROUNDS, NZ)),
            dma((ROUNDS - 1, NZ)),
            dma((ROUNDS - 1,)),
            dma((ROUNDS,)),
            dma((ROUNDS,)),
            dma((ROUNDS,)),
            dma((ROUNDS,)),
        ],
        compiler_params=pltpu.CompilerParams(
            collective_id=0, has_side_effects=True, vmem_limit_bytes=48 * 1024 * 1024
        ),
        name="conjugate_gradients",
    )(genotype, pheno_probes, centre.reshape(1, COLS), spread.reshape(1, COLS))


def solution(mesh):
    in_specs = (P("samp", "snp"), P("snp"), P("snp"), P(None, ("samp", "snp")))
    out_specs = (P(None, ("samp", "snp")), P(None, "snp"))
    return jax.shard_map(local, mesh=mesh, in_specs=in_specs, out_specs=out_specs, check_vma=False)
```

time: 464 us -> 107 us (0.23)
  blocking collectives: 228 us -> 0 us
  matrix products: 134 us -> 0 us
  Pallas kernels: 0 us -> 103 us
  starting transfers between devices: 31.5 us -> 0 us
  other arithmetic: 29.5 us -> 0 us
  waiting for transfers between devices: 28 us -> 0 us
  local copies, waits for them, and re-layouts: 10.5 us -> 3.44 us
    all_to_all x11 -> x0, blocking collectives: 228 us -> none  [the longest x8 164 us: sent_to_all(): return lax.all_to_all(copies, axis, split_axis=0, concat_axis=0, tiled=True)]
    dot_general x6 -> x0, matrix products: 134 us -> none  [the longest x3 79.7 us: operate(): lax.dot_general(marker_load, scores, (((1,), (1,)), ((), ())), precision=...]
    pallas_call x0 -> x1, Pallas kernels: none -> 103 us  [local(): pl.pallas_call(kernel, out_shape=(jax.ShapeDtypeStruct((ROWS, 160), f32),...]
    all_to_all x5 -> x0, starting transfers between devices: 31.5 us -> none  [sent_to_all(): return lax.all_to_all(copies, axis, split_axis=0, concat_axis=0, tiled=True)]
    all_to_all x5 -> x0, waiting for transfers between devices: 28 us -> none  [sent_to_all(): return lax.all_to_all(copies, axis, split_axis=0, concat_axis=0, tiled=True)]
    div x8 -> x0, other arithmetic: 18 us -> none  [the longest x1 14.8 us: local(): scores = (genotype.astype(jnp.float32) - centre[None, :]) / spread[None, :]]
    add x6 -> x0, other arithmetic: 6.9 us -> none  [the longest x2 4.02 us: combined_update(): stats_total = stats_total + step_size * dir_loads]
    broadcast_in_dim x13 -> x0, local copies, waits for them, and re-layouts: 5.56 us -> none  [sent_to_all(): copies = jnp.broadcast_to(array, (lax.axis_size(axis), *array.shape))]
  transfers between devices with their start and end apart: 5 -> 0, of which waited for: 5 -> 0; matrix products, arithmetic and copies ran while one was open for 3% -> 0% of each run, Pallas kernels for 0% -> 0%
where the time goes in v1:
time: 107 us
  Pallas kernels  103 us (96%)
  local copies, waits for them, and re-layouts  3.44 us (3%)
    pallas_call x1, Pallas kernels, local(): pl.pallas_call(kernel, out_shape=(jax.ShapeDtypeStruct((ROWS, 160), f32),...  103 us

profile of v1, /device:TPU:1, one launch (start us, length us, event | category | flops | bytes accessed | tf_op | source)
XLA Modules:
  0.0 106.6 jit_solution(5200990925650048334)
XLA Ops:
  0.6 0.7 reshape.10.centre_ref
  1.3 0.7 reshape.11.spread_ref
  2.0 0.0 copy-start
  2.0 0.8 copy-done
  2.8 102.5 %conjugate_gradients.1 = (f32[32,160]{1,0:T(8,128)S(1)}, f32[32,1280]{1,0:T(8,128)S(1)}) custom-call(bf16[5120,1280]{1,0:T(8,128)(2,1)} %geno_hbm.1, f32[32,160]{1,0:T(8,128)S(1)} %copy-done, f32[1,1280]{1,0:T(1,128)S(1)} %reshape.10.centre_ref, f32[1,1280]{1,0:T(1,128)S(1)} %reshape.11.spread_ref), custom_call_target="tpu_custom_call" | custom-call | tf_op jit(solution)/shard_map/conjugate_gradients/pallas_call | solution.py:347
  105.3 0.6 copy.8
  105.9 0.7 copy.9
Async XLA Ops:
  2.0 0.8 copy-start

commit v2 on v1

--- a/solution.py
+++ b/solution.py
@@ -23,13 +23,21 @@
 PIECE = 8 * CHUNK
 
 MESH = pl.DeviceIdType.MESH
-NEAR = (1, 7, 2, 6, 3, 5, 4)
+FAR = (2, 6, 3, 5, 4)
+SCATTER = (4, 3, 5, 1, 7, 2, 6, 0)
 f32 = jnp.float32
 
 
 def near(step):
     half = (step + 1) // 2
     return jnp.where(step % 2 == 1, half, (NZ - half) % NZ)
+
+
+def scatter_order(step):
+    offset = jnp.int32(SCATTER[0])
+    for place in range(1, NZ):
+        offset = jnp.where(step == place, SCATTER[place], offset)
+    return offset
 
 
 def split(value):
@@ -46,12 +54,12 @@
 
 
 def kernel(
-    geno_hbm, rhs_ref, centre_ref, spread_ref, solution_ref, stats_ref,
+    geno_hbm, rhs_hbm, centre_hbm, spread_hbm, solution_ref, stats_ref,
     geno, r_0, r_1, r_2, packed, u_0, u_1, from_y_0, from_y_1, to_z_0, to_z_1,
     from_z_0, from_z_1, partial, acc, loads_out, from_core, by_x, loads_in,
     scalars, lhs, dir_loads, steps, betas,
-    geno_sem, s_gz, s_gy, s_ry, s_rz, s_core, s_x, s_back, s_sc,
-    gz, gy, ry, rz, core_sem, x_sem, back_sem, sc_sem,
+    from_side, turned, rhs_ref, centre_ref, spread_ref, small_sem, geno_sem, s_gz, s_gy, s_gn, s_ry, s_rn, s_rz, s_core, s_x, s_back, s_sc,
+    gz, gy, ry, rn, rz, core_sem, x_sem, back_sem, sc_sem,
 ):
     samp, snp = lax.axis_index("samp"), lax.axis_index("snp")
     x, core = samp // 2, samp % 2
@@ -77,6 +85,7 @@
     def settle(sem, like):
         pltpu.make_async_copy(like, like, sem).wait()
 
+    piece = r_0.at[0:8, 0:CHUNK]
     pieces = r_0.at[0:24, 0:CHUNK]
 
     def rows_of(group):
@@ -85,6 +94,33 @@
     def cols_of(chunk):
         return pl.ds(pl.multiple_of(chunk * CHUNK, 128), CHUNK)
 
+    barrier = pltpu.get_barrier_semaphore()
+
+    def greet(offset, carry):
+        pl.semaphore_signal(
+            barrier, inc=1, device_id=(samp, (snp + offset) % PEERS), device_id_type=MESH
+        )
+        return carry
+
+    lax.fori_loop(1, PEERS, greet, 0)
+    pl.semaphore_signal(barrier, inc=1, device_id=partner, device_id_type=MESH)
+    for dx in range(1, NX):
+        pl.semaphore_signal(barrier, inc=1, device_id=at_x((x + dx) % NX), device_id_type=MESH)
+
+    small = (
+        (rhs_hbm, rhs_ref), (centre_hbm, centre_ref.at[0]), (spread_hbm, spread_ref.at[0])
+    )
+    for which, (source, target) in enumerate(small):
+        pltpu.make_async_copy(source, target, small_sem.at[which]).start()
+
+    def main_cols(yy, zz):
+        return pl.ds(pl.multiple_of(zz * CHUNK + yy * 128, 128), 128)
+
+    for which, (source, target) in enumerate(small):
+        pltpu.make_async_copy(source, target, small_sem.at[which]).wait()
+    r_0[:, main_cols(y, z)] = rhs_ref[:, 0:128]
+    tails = [rhs_ref[8 * group : 8 * group + 8, 128:160] for group in range(4)]
+    packed[y, z] = jnp.concatenate(tails, axis=1)
     for zz in range(NZ):
         for yy in range(NY):
             first = 160 * (yy * NZ + zz)
@@ -97,52 +133,38 @@
                 geno_sem,
             ).start()
 
-    barrier = pltpu.get_barrier_semaphore()
-
-    def greet(offset, carry):
-        pl.semaphore_signal(
-            barrier, inc=1, device_id=(samp, (snp + offset) % PEERS), device_id_type=MESH
-        )
-        return carry
-
-    lax.fori_loop(1, PEERS, greet, 0)
-    pl.semaphore_signal(barrier, inc=1, device_id=partner, device_id_type=MESH)
-    for dx in range(1, NX):
-        pl.semaphore_signal(barrier, inc=1, device_id=at_x((x + dx) % NX), device_id_type=MESH)
-
-    def main_cols(zz):
-        return pl.ds(pl.multiple_of(zz * CHUNK + y * 128, 128), 128)
-
-    r_0[:, main_cols(z)] = rhs_ref[:, 0:128]
-    tails = [rhs_ref[8 * group : 8 * group + 8, 128:160] for group in range(4)]
-    packed[y, z] = jnp.concatenate(tails, axis=1)
     pl.semaphore_wait(barrier, PEERS - 1 + NX)
 
-    def forward_own(k, zz):
+    def send_piece(k, yy, zz, send_sem, recv_sem, device):
+        if k == 0:
+            block = r_0.at[:, main_cols(yy, zz)]
+            send(block, block, send_sem, recv_sem, device)
+            send(packed.at[yy, zz], packed.at[yy, zz], send_sem, recv_sem, device)
+        else:
+            block = residuals[k].at[rows_of(yy), cols_of(zz)]
+            send(block, block, send_sem, recv_sem, device)
+
+    def forward(k, zz):
+        for dy in (2, 1, 3):
+            send_piece(k, y, zz, s_gy.at[k], gy.at[k, zz], at_y((y + dy) % NY))
+
+    def pass_forward(k, d):
+        settle(gz.at[k, d - 1], piece)
+        forward(k, (z - d + NZ) % NZ)
+
+    def gather(k):
+        forward(k, z)
+        for d in FAR + (1, 7):
+            send_piece(k, y, z, s_gz.at[k], gz.at[k, d - 1], at_z((z + d) % NZ))
+        settle(gy.at[k, z], pieces)
         for dy in range(1, NY):
-            other = at_y((y + dy) % NY)
-            if k == 0:
-                block = r_0.at[:, main_cols(zz)]
-                send(block, block, s_gy.at[0], gy.at[0, zz], other)
-                send(packed.at[y, zz], packed.at[y, zz], s_gy.at[0], gy.at[0, zz], other)
-            else:
-                block = residuals[k].at[rows_of(y), cols_of(zz)]
-                send(block, block, s_gy.at[k], gy.at[k, zz], other)
-
-    def gather(k):
-        for d in NEAR:
-            other = at_z((z + d) % NZ)
-            if k == 0:
-                block = r_0.at[:, main_cols(z)]
-                send(block, block, s_gz.at[0], gz.at[0, d - 1], other)
-                send(packed.at[y, z], packed.at[y, z], s_gz.at[0], gz.at[0, d - 1], other)
-            else:
-                block = residuals[k].at[rows_of(y), cols_of(z)]
-                send(block, block, s_gz.at[k], gz.at[k, d - 1], other)
-        forward_own(k, z)
-        for d in NEAR:
-            settle(gz.at[k, d - 1], r_0.at[0:8, 0:CHUNK])
-            forward_own(k, (z - d + NZ) % NZ)
+            for d in (1, 7):
+                other = at_z((z + d) % NZ)
+                send_piece(k, (y + dy) % NY, z, s_gn.at[k], gy.at[k, z], other)
+        partial[...] = jnp.zeros_like(partial)
+        acc[...] = jnp.zeros_like(acc)
+        for d in FAR[:2]:
+            pass_forward(k, d)
 
     lane = lax.broadcasted_iota(jnp.int32, (8, 128), 1)
 
@@ -157,34 +179,49 @@
             start = pl.multiple_of(zz * CHUNK + 512, 128)
             r_0[8 * group : 8 * group + 8, pl.ds(start, 128)] = tile
 
+    def multiply_in(k, zz):
+        if k == 0:
+            unpack(zz)
+        value = residuals[k][:, cols_of(zz)]
+        high, low = split(value)
+        partial[...] += jnp.dot(
+            jnp.concatenate([high, low], axis=0), geno[cols_of(zz), :], preferred_element_type=f32
+        )
+        acc[0] += lanes_summed(high.astype(f32) + low.astype(f32))
+        acc[1] += lanes_summed(value * value)
+        if k > 0:
+            acc[2] += lanes_summed(value * residuals[k - 1][:, cols_of(zz)])
+        if k > 1:
+            acc[3] += lanes_summed(value * r_0[:, cols_of(zz)])
+
     def to_loads(k):
-        partial[...] = jnp.zeros_like(partial)
-        acc[...] = jnp.zeros_like(acc)
-
         def chunk(step, carry):
             zz = (z - near(step) + NZ) % NZ
-            settle(gy.at[k, zz], pieces)
-            if k == 0:
-                unpack(zz)
-            value = residuals[k][:, cols_of(zz)]
-            high, low = split(value)
-            partial[...] += jnp.dot(
-                jnp.concatenate([high, low], axis=0),
-                geno[cols_of(zz), :],
-                preferred_element_type=f32,
-            )
-            acc[0] += lanes_summed(high.astype(f32) + low.astype(f32))
-            acc[1] += lanes_summed(value * value)
-            if k > 0:
-                acc[2] += lanes_summed(value * residuals[k - 1][:, cols_of(zz)])
-            if k > 1:
-                acc[3] += lanes_summed(value * r_0[:, cols_of(zz)])
+
+            @pl.when(step > 0)
+            def _():
+                settle(gy.at[k, zz], pieces)
+
+            multiply_in(k, zz)
+
+            @pl.when(step == 0)
+            def _():
+                for d in FAR[2:]:
+                    pass_forward(k, d)
+                for d in (1, 7):
+                    settle(gz.at[k, d - 1], piece)
+
             return carry
 
         lax.fori_loop(0, NZ, chunk, 0)
 
     lane32 = lax.broadcasted_iota(jnp.int32, (ROWS, 128), 1)
     eye = lax.broadcasted_iota(jnp.int32, (ROWS, 128), 0) == lane32
+
+    def turn(zz, carry):
+        for first in range(0, COLS, 256):
+            turned[first : first + 256, cols_of(zz)] = geno[cols_of(zz), first : first + 256].T
+        return carry
 
     def over_samp(k):
         out, got, halves, full = loads_out.at[k], from_core.at[k], by_x.at[k], loads_in.at[k]
@@ -202,6 +239,8 @@
         halves[x] = out[mine, :] + got[...]
         for dx in (2, 1, 3):
             send(halves.at[x], halves.at[x], s_x.at[k], x_sem.at[k], at_x((x + dx) % NX))
+        if k == 0:
+            lax.fori_loop(0, NZ, turn, 0)
         settle(x_sem.at[k], halves.at[0:3])
         full[mine, :] = (halves[0] + halves[1]) + (halves[2] + halves[3])
         send(full.at[mine], full.at[mine], s_back.at[k], back_sem.at[k], partner)
@@ -213,12 +252,12 @@
         row = jnp.sum(jnp.where(eye, norm, 0.0), axis=0, keepdims=True)
         scalars[k, snp] = row
 
-        def one(offset, carry):
-            slot = scalars.at[k, snp]
-            send(slot, slot, s_sc.at[k], sc_sem.at[k], (samp, (snp + offset) % PEERS))
-            return carry
-
-        lax.fori_loop(1, PEERS, one, 0)
+        slot = scalars.at[k, snp]
+        for dz in (4, 3, 5, 2, 6, 1, 7, 0):
+            for dy in (2, 1, 3, 0):
+                if dy or dz:
+                    other = (samp, (y + dy) % NY * NZ + (z + dz) % NZ)
+                    send(slot, slot, s_sc.at[k], sc_sem.at[k], other)
 
     def total_norms(k):
         settle(sc_sem.at[k], scalars.at[k, 0 : PEERS - 1])
@@ -235,43 +274,64 @@
         shift = (high.astype(f32) + low.astype(f32)) * centre_ref[...]
         shift = jnp.sum(lanes_summed(shift), axis=1, keepdims=True)
 
-        def chunk(step, carry):
-            zz = (z + near(NZ - 1 - step)) % NZ
-            both = lax.dot_general(
-                lhs[...], geno[cols_of(zz), :], (((1,), (1,)), ((), ())),
-                preferred_element_type=f32,
-            )
+        def multiply(offset):
+            zz = (z + offset) % NZ
+            both = jnp.dot(lhs[...], turned[:, cols_of(zz)], preferred_element_type=f32)
             image[:, cols_of(zz)] = both[0:ROWS] + both[ROWS : 2 * ROWS] - shift
-            for dy in range(1, NY):
+
+        def along_y(zz):
+            for dy in (2, 1, 3):
                 other = (y + dy) % NY
                 send(
                     image.at[rows_of(other), cols_of(zz)], from_y.at[dy - 1, :, cols_of(zz)],
                     s_ry.at[k], ry.at[k, zz], at_y(other),
                 )
+
+        def chunk(step, carry):
+            offset = scatter_order(step)
+            multiply(offset)
+            zz = (z + offset) % NZ
+            beside = (offset == 1) | (offset == 7)
+
+            @pl.when(beside)
+            def _():
+                send(
+                    image.at[:, cols_of(zz)], from_side.at[k, offset // 4],
+                    s_rn.at[k], rn.at[k], at_z(zz),
+                )
+
+            @pl.when((offset != 0) & ~beside)
+            def _():
+                along_y(zz)
+
             return carry
 
         lax.fori_loop(0, NZ, chunk, 0)
-
-        def pass_on(step, carry):
-            offset = near(NZ - 1 - step)
-            zz = (z + offset) % NZ
+        spread_norms(k)
+
+        def of_y(zz):
             settle(ry.at[k, zz], pieces)
             total = image[rows_of(y), cols_of(zz)]
             for dy in range(NY - 1):
                 total = total + from_y[dy, :, cols_of(zz)]
-            to_z[zz] = total
-
-            @pl.when(step < NZ - 1)
-            def _():
-                send(to_z.at[zz], from_z.at[offset - 1], s_rz.at[k], rz.at[k], at_z(zz))
-
-            return carry
-
-        lax.fori_loop(0, NZ, pass_on, 0)
+            return total
+
+        def pass_on(offset):
+            zz = (z + offset) % NZ
+            to_z[zz] = of_y(zz)
+            send(to_z.at[zz], from_z.at[offset - 2], s_rz.at[k], rz.at[k], at_z(zz))
+
+        for offset in (4, 3, 5):
+            pass_on(offset)
+        settle(rn.at[k], from_side.at[k])
+        image[:, cols_of(z)] += from_side[k, 0] + from_side[k, 1]
+        along_y(z)
+        for offset in (2, 6):
+            pass_on(offset)
+        total = of_y(z)
         settle(rz.at[k], from_z)
-        total = to_z[z]
-        for d in range(NZ - 1):
-            total = total + from_z[d]
+        for slot in range(NZ - 3):
+            total = total + from_z[slot]
         return total
 
     norms, squares = [], []
@@ -296,9 +356,10 @@
             betas[k - 1] = jnp.broadcast_to(beta, (ROWS, 128))
         norms.append(norm)
         squares.append(square)
-        spread_norms(k)
         if k < ROUNDS - 1:
             summed = to_image(k)
+        else:
+            spread_norms(k)
         size = norm / (total_norms(k) * (1.0 / MARKERS) + RIDGE * square)
         steps[k] = jnp.broadcast_to(size, (ROWS, 128))
         gain = size * (1.0 / math.sqrt(SAMPLES))
@@ -320,7 +381,7 @@
         third = r_2[:, columns] + betas[1][:, 0:1] * second
         return steps[0][:, 0:1] * first + steps[1][:, 0:1] * second + steps[2][:, 0:1] * third
 
-    solution_ref[:, 0:128] = combined(main_cols(z))
+    solution_ref[:, 0:128] = combined(main_cols(y, z))
     tail = combined(pl.ds(pl.multiple_of(z * CHUNK + 512, 128), 128))
     for yy in range(NY):
 
@@ -329,14 +390,16 @@
             solution_ref[:, 128:160] = tail[:, 32 * yy : 32 * yy + 32]
 
     for k in range(ROUNDS):
-        settle(s_gz.at[k], from_z_0)
-        settle(s_gy.at[k], r_0.at[0:24])
+        settle(s_gz.at[k], r_0.at[0:8, 0 : 7 * CHUNK])
+        settle(s_gy.at[k], r_0.at[0:24, 0 : 6 * CHUNK])
+        settle(s_gn.at[k], r_0.at[0:24, 0 : 2 * CHUNK])
         settle(s_core.at[k], from_core.at[k])
         settle(s_x.at[k], by_x.at[k, 0:3])
         settle(s_back.at[k], from_core.at[k])
         settle(s_sc.at[k], scalars.at[k, 0 : PEERS - 1])
     for k in range(ROUNDS - 1):
-        settle(s_ry.at[k], r_0.at[0:24])
+        settle(s_ry.at[k], r_0.at[0:24, 0 : 6 * CHUNK])
+        settle(s_rn.at[k], from_side.at[k])
         settle(s_rz.at[k], from_z_0)
 
 
@@ -350,7 +413,7 @@
             jax.ShapeDtypeStruct((ROWS, 160), f32),
             jax.ShapeDtypeStruct((ROWS, COLS), f32),
         ),
-        in_specs=[pl.BlockSpec(memory_space=pl.ANY), vmem, vmem, vmem],
+        in_specs=[pl.BlockSpec(memory_space=pl.ANY)] * 4,
         out_specs=(vmem, vmem),
         scratch_shapes=[
             pltpu.VMEM((BLOCK, COLS), jnp.bfloat16),
@@ -364,8 +427,8 @@
             pltpu.VMEM((NY - 1, 8, BLOCK), f32),
             pltpu.VMEM((NZ, 8, CHUNK), f32),
             pltpu.VMEM((NZ, 8, CHUNK), f32),
-            pltpu.VMEM((NZ - 1, 8, CHUNK), f32),
-            pltpu.VMEM((NZ - 1, 8, CHUNK), f32),
+            pltpu.VMEM((NZ - 3, 8, CHUNK), f32),
+            pltpu.VMEM((NZ - 3, 8, CHUNK), f32),
             pltpu.VMEM((2 * ROWS, COLS), f32),
             pltpu.VMEM((4, ROWS, 128), f32),
             pltpu.VMEM((ROUNDS, ROWS, WIDE), f32),
@@ -377,9 +440,17 @@
             pltpu.VMEM((ROWS, COLS), f32),
             pltpu.VMEM((ROUNDS, ROWS, 128), f32),
             pltpu.VMEM((ROUNDS - 1, ROWS, 128), f32),
+            pltpu.VMEM((ROUNDS - 1, 2, ROWS, CHUNK), f32),
+            pltpu.VMEM((COLS, BLOCK), jnp.bfloat16),
+            pltpu.VMEM((ROWS, 160), f32),
+            pltpu.VMEM((1, COLS), f32),
+            pltpu.VMEM((1, COLS), f32),
+            dma((3,)),
             dma,
             dma((ROUNDS,)),
             dma((ROUNDS,)),
+            dma((ROUNDS,)),
+            dma((ROUNDS - 1,)),
             dma((ROUNDS - 1,)),
             dma((ROUNDS - 1,)),
             dma((ROUNDS,)),
@@ -390,16 +461,17 @@
             dma((ROUNDS, NZ)),
             dma((ROUNDS - 1, NZ)),
             dma((ROUNDS - 1,)),
+            dma((ROUNDS - 1,)),
             dma((ROUNDS,)),
             dma((ROUNDS,)),
             dma((ROUNDS,)),
             dma((ROUNDS,)),
         ],
         compiler_params=pltpu.CompilerParams(
-            collective_id=0, has_side_effects=True, vmem_limit_bytes=48 * 1024 * 1024
+            collective_id=0, has_side_effects=True, vmem_limit_bytes=60 * 1024 * 1024
         ),
         name="conjugate_gradients",
-    )(genotype, pheno_probes, centre.reshape(1, COLS), spread.reshape(1, COLS))
+    )(genotype, pheno_probes, centre, spread)
 
 
 def solution(mesh):

time: 107 us -> 101 us (0.944)
  Pallas kernels: 103 us -> 97.4 us
    pallas_call x1, Pallas kernels: 103 us -> 97.4 us  [local(): pl.pallas_call(kernel, out_shape=(jax.ShapeDtypeStruct((ROWS, 160), f32),...]
    reshape x2 -> x0, local copies, waits for them, and re-layouts: 1.4 us -> none  [the longest x1 0.7 us: local(): centre.reshape(1, COLS)]
    unnamed x4 -> x2, local copies, waits for them, and re-layouts: 2.04 us -> 2.97 us
where the time goes in v2:
time: 101 us
  Pallas kernels  97.4 us (96%)
  local copies, waits for them, and re-layouts  2.97 us (3%)
    pallas_call x1, Pallas kernels, local(): pl.pallas_call(kernel, out_shape=(jax.ShapeDtypeStruct((ROWS, 160), f32),...  97.4 us
    unnamed x2, local copies, waits for them, and re-layouts  2.97 us

profile of v2, /device:TPU:1, one launch (start us, length us, event | category | flops | bytes accessed | tf_op | source)
XLA Modules:
  0.0 101.0 jit_solution(3794291853432027966)
XLA Ops:
  0.6 97.4 %conjugate_gradients.1 = (f32[32,160]{1,0:T(8,128)}, f32[32,1280]{1,0:T(8,128)}) custom-call(bf16[5120,1280]{1,0:T(8,128)(2,1)} %geno_hbm.1, f32[32,160]{1,0:T(8,128)} %rhs_hbm.1, f32[1280]{0:T(1024)} %centre_hbm.1, f32[1280]{0:T(1024)} %spread_hbm.1), custom_call_target="tpu_custom_call" | custom-call | tf_op jit(solution)/shard_map/conjugate_gradients/pallas_call | solution.py:410
  98.1 1.4 %copy.8 = f32[32,160]{1,0:T(8,128)} copy(f32[32,160]{1,0:T(8,128)} %get-tuple-element.4) | data formatting | bytes 40960
  99.5 1.6 %copy.9 = f32[32,1280]{1,0:T(8,128)} copy(f32[32,1280]{1,0:T(8,128)} %get-tuple-element.5) | data formatting | bytes 327680

commit v3 on v2

--- a/solution.py
+++ b/solution.py
@@ -96,17 +96,12 @@
 
     barrier = pltpu.get_barrier_semaphore()
 
-    def greet(offset, carry):
-        pl.semaphore_signal(
-            barrier, inc=1, device_id=(samp, (snp + offset) % PEERS), device_id_type=MESH
-        )
-        return carry
-
-    lax.fori_loop(1, PEERS, greet, 0)
-    pl.semaphore_signal(barrier, inc=1, device_id=partner, device_id_type=MESH)
-    for dx in range(1, NX):
-        pl.semaphore_signal(barrier, inc=1, device_id=at_x((x + dx) % NX), device_id_type=MESH)
-
+    greeted = [at_z((z + d) % NZ) for d in (4, 3, 5, 2, 6)]
+    greeted += [at_y((y + dy) % NY) for dy in (2, 1, 3)]
+    greeted += [at_x((x + dx) % NX) for dx in (2, 1, 3)]
+    greeted += [at_z((z + d) % NZ) for d in (1, 7)] + [partner]
+    for other in greeted:
+        pl.semaphore_signal(barrier, inc=1, device_id=other, device_id_type=MESH)
     small = (
         (rhs_hbm, rhs_ref), (centre_hbm, centre_ref.at[0]), (spread_hbm, spread_ref.at[0])
     )
@@ -133,7 +128,7 @@
                 geno_sem,
             ).start()
 
-    pl.semaphore_wait(barrier, PEERS - 1 + NX)
+    pl.semaphore_wait(barrier, len(greeted))
 
     def send_piece(k, yy, zz, send_sem, recv_sem, device):
         if k == 0:

time: 101 us -> 100 us (0.990)
  Pallas kernels: 97.4 us -> 96.2 us
    pallas_call x1, Pallas kernels: 97.4 us -> 96.2 us  [local(): pl.pallas_call(kernel, out_shape=(jax.ShapeDtypeStruct((ROWS, 160), f32),...]
where the time goes in v3:
time: 100 us; the launch traced here: 99.8 us
  Pallas kernels  96.2 us (96%)
  local copies, waits for them, and re-layouts  2.97 us (3%)
    pallas_call x1, Pallas kernels, local(): pl.pallas_call(kernel, out_shape=(jax.ShapeDtypeStruct((ROWS, 160), f32),...  96.2 us
    unnamed x2, local copies, waits for them, and re-layouts  2.97 us

profile of v3, /device:TPU:1, one launch (start us, length us, event | category | flops | bytes accessed | tf_op | source)
XLA Modules:
  0.0 99.8 jit_solution(11409422198305962234)
XLA Ops:
  0.6 96.2 %conjugate_gradients.1 = (f32[32,160]{1,0:T(8,128)}, f32[32,1280]{1,0:T(8,128)}) custom-call(bf16[5120,1280]{1,0:T(8,128)(2,1)} %geno_hbm.1, f32[32,160]{1,0:T(8,128)} %rhs_hbm.1, f32[1280]{0:T(1024)} %centre_hbm.1, f32[1280]{0:T(1024)} %spread_hbm.1), custom_call_target="tpu_custom_call" | custom-call | tf_op jit(solution)/shard_map/conjugate_gradients/pallas_call | solution.py:405
  96.9 1.4 %copy.8 = f32[32,160]{1,0:T(8,128)} copy(f32[32,160]{1,0:T(8,128)} %get-tuple-element.4) | data formatting | bytes 40960
  98.2 1.6 %copy.9 = f32[32,1280]{1,0:T(8,128)} copy(f32[32,1280]{1,0:T(8,128)} %get-tuple-element.5) | data formatting | bytes 327680

commit v4 on v3

--- a/solution.py
+++ b/solution.py
@@ -58,7 +58,7 @@
     geno, r_0, r_1, r_2, packed, u_0, u_1, from_y_0, from_y_1, to_z_0, to_z_1,
     from_z_0, from_z_1, partial, acc, loads_out, from_core, by_x, loads_in,
     scalars, lhs, dir_loads, steps, betas,
-    from_side, turned, rhs_ref, centre_ref, spread_ref, small_sem, geno_sem, s_gz, s_gy, s_gn, s_ry, s_rn, s_rz, s_core, s_x, s_back, s_sc,
+    last, from_side, turned, rhs_ref, centre_ref, spread_ref, small_sem, geno_sem, s_gz, s_gy, s_gn, s_ry, s_rn, s_rz, s_core, s_x, s_back, s_sc,
     gz, gy, ry, rn, rz, core_sem, x_sem, back_sem, sc_sem,
 ):
     samp, snp = lax.axis_index("samp"), lax.axis_index("snp")
@@ -239,7 +239,27 @@
         settle(x_sem.at[k], halves.at[0:3])
         full[mine, :] = (halves[0] + halves[1]) + (halves[2] + halves[3])
         send(full.at[mine], full.at[mine], s_back.at[k], back_sem.at[k], partner)
+        if k == ROUNDS - 1:
+            spread_halves(mine)
         settle(back_sem.at[k], full.at[mine])
+
+    def spread_halves(mine):
+        k = ROUNDS - 1
+        half = loads_in[k, mine, :]
+        beta = half[:, COLS : COLS + 1] / loads_in[k - 1, mine, COLS : COLS + 1]
+        loads = half[:, 0:COLS] + beta * dir_loads[mine, :]
+        norm = jnp.sum(lanes_summed(loads * loads), axis=1, keepdims=True)
+        place = lax.broadcasted_iota(jnp.int32, (16, 128), 0) + 16 * core
+        here = place == lax.broadcasted_iota(jnp.int32, (16, 128), 1)
+        at = core * PEERS + snp
+        last[at] = jnp.sum(jnp.where(here, norm, 0.0), axis=0, keepdims=True)
+        slot = last.at[at]
+        for dz in (4, 3, 5, 2, 6, 1, 7, 0):
+            for dy in (2, 1, 3, 0):
+                peer = (y + dy) % NY * NZ + (z + dz) % NZ
+                if dy or dz:
+                    send(slot, slot, s_sc.at[k], sc_sem.at[k], (samp, peer))
+                send(slot, slot, s_sc.at[k], sc_sem.at[k], (x * 2 + 1 - core, peer))
 
     def spread_norms(k):
         loads = dir_loads[...]
@@ -255,8 +275,12 @@
                     send(slot, slot, s_sc.at[k], sc_sem.at[k], other)
 
     def total_norms(k):
-        settle(sc_sem.at[k], scalars.at[k, 0 : PEERS - 1])
-        row = jnp.sum(scalars[k], axis=0)
+        if k == ROUNDS - 1:
+            settle(sc_sem.at[k], last.at[0 : 2 * PEERS - 1])
+            row = jnp.sum(last[...], axis=0)
+        else:
+            settle(sc_sem.at[k], scalars.at[k, 0 : PEERS - 1])
+            row = jnp.sum(scalars[k], axis=0)
         return jnp.sum(jnp.where(eye, row, 0.0), axis=1, keepdims=True)
 
     def to_image(k):
@@ -353,8 +377,6 @@
         squares.append(square)
         if k < ROUNDS - 1:
             summed = to_image(k)
-        else:
-            spread_norms(k)
         size = norm / (total_norms(k) * (1.0 / MARKERS) + RIDGE * square)
         steps[k] = jnp.broadcast_to(size, (ROWS, 128))
         gain = size * (1.0 / math.sqrt(SAMPLES))
@@ -391,8 +413,9 @@
         settle(s_core.at[k], from_core.at[k])
         settle(s_x.at[k], by_x.at[k, 0:3])
         settle(s_back.at[k], from_core.at[k])
+    settle(s_sc.at[ROUNDS - 1], last.at[0 : 2 * PEERS - 1])
+    for k in range(ROUNDS - 1):
         settle(s_sc.at[k], scalars.at[k, 0 : PEERS - 1])
-    for k in range(ROUNDS - 1):
         settle(s_ry.at[k], r_0.at[0:24, 0 : 6 * CHUNK])
         settle(s_rn.at[k], from_side.at[k])
         settle(s_rz.at[k], from_z_0)
@@ -430,11 +453,12 @@
             pltpu.VMEM((ROUNDS, 16, WIDE), f32),
             pltpu.VMEM((ROUNDS, NX, 16, WIDE), f32),
             pltpu.VMEM((ROUNDS, ROWS, WIDE), f32),
-            pltpu.VMEM((ROUNDS, PEERS, 1, 128), f32),
+            pltpu.VMEM((ROUNDS - 1, PEERS, 1, 128), f32),
             pltpu.VMEM((2 * ROWS, COLS), jnp.bfloat16),
             pltpu.VMEM((ROWS, COLS), f32),
             pltpu.VMEM((ROUNDS, ROWS, 128), f32),
             pltpu.VMEM((ROUNDS - 1, ROWS, 128), f32),
+            pltpu.VMEM((2 * PEERS, 1, 128), f32),
             pltpu.VMEM((ROUNDS - 1, 2, ROWS, CHUNK), f32),
             pltpu.VMEM((COLS, BLOCK), jnp.bfloat16),
             pltpu.VMEM((ROWS, 160), f32),

time: 100 us -> 99.7 us (level)
  no operation moved by 1% of the time
where the time goes in v4:
time: 99.7 us; the launch traced here: 99.4 us
  Pallas kernels  95.8 us (96%)
  local copies, waits for them, and re-layouts  2.97 us (3%)
    pallas_call x1, Pallas kernels, local(): pl.pallas_call(kernel, out_shape=(jax.ShapeDtypeStruct((ROWS, 160), f32),...  95.8 us
    unnamed x2, local copies, waits for them, and re-layouts  2.97 us

profile of v4, /device:TPU:1, one launch (start us, length us, event | category | flops | bytes accessed | tf_op | source)
XLA Modules:
  0.0 99.4 jit_solution(11530203160890056969)
XLA Ops:
  0.6 95.8 %conjugate_gradients.1 = (f32[32,160]{1,0:T(8,128)}, f32[32,1280]{1,0:T(8,128)}) custom-call(bf16[5120,1280]{1,0:T(8,128)(2,1)} %geno_hbm.1, f32[32,160]{1,0:T(8,128)} %rhs_hbm.1, f32[1280]{0:T(1024)} %centre_hbm.1, f32[1280]{0:T(1024)} %spread_hbm.1), custom_call_target="tpu_custom_call" | custom-call | tf_op jit(solution)/shard_map/conjugate_gradients/pallas_call | solution.py:428
  96.5 1.4 %copy.8 = f32[32,160]{1,0:T(8,128)} copy(f32[32,160]{1,0:T(8,128)} %get-tuple-element.4) | data formatting | bytes 40960
  97.8 1.6 %copy.9 = f32[32,1280]{1,0:T(8,128)} copy(f32[32,1280]{1,0:T(8,128)} %get-tuple-element.5) | data formatting | bytes 327680

commit v5 on v4

--- a/solution.py
+++ b/solution.py
@@ -340,12 +340,12 @@
             to_z[zz] = of_y(zz)
             send(to_z.at[zz], from_z.at[offset - 2], s_rz.at[k], rz.at[k], at_z(zz))
 
-        for offset in (4, 3, 5):
+        for offset in (4, 3, 5, 2):
             pass_on(offset)
         settle(rn.at[k], from_side.at[k])
         image[:, cols_of(z)] += from_side[k, 0] + from_side[k, 1]
         along_y(z)
-        for offset in (2, 6):
+        for offset in (6,):
             pass_on(offset)
         total = of_y(z)
         settle(rz.at[k], from_z)

time: 99.7 us -> 99.2 us (level)
  no operation moved by 1% of the time
where the time goes in v5:
time: 99.2 us; the launch traced here: 99 us
  Pallas kernels  95.4 us (96%)
  local copies, waits for them, and re-layouts  2.97 us (3%)
    pallas_call x1, Pallas kernels, local(): pl.pallas_call(kernel, out_shape=(jax.ShapeDtypeStruct((ROWS, 160), f32),...  95.4 us
    unnamed x2, local copies, waits for them, and re-layouts  2.97 us

profile of v5, /device:TPU:1, one launch (start us, length us, event | category | flops | bytes accessed | tf_op | source)
XLA Modules:
  0.0 99.0 jit_solution(5070595689628815538)
XLA Ops:
  0.6 95.4 %conjugate_gradients.1 = (f32[32,160]{1,0:T(8,128)}, f32[32,1280]{1,0:T(8,128)}) custom-call(bf16[5120,1280]{1,0:T(8,128)(2,1)} %geno_hbm.1, f32[32,160]{1,0:T(8,128)} %rhs_hbm.1, f32[1280]{0:T(1024)} %centre_hbm.1, f32[1280]{0:T(1024)} %spread_hbm.1), custom_call_target="tpu_custom_call" | custom-call | tf_op jit(solution)/shard_map/conjugate_gradients/pallas_call | solution.py:428
  96.0 1.4 %copy.8 = f32[32,160]{1,0:T(8,128)} copy(f32[32,160]{1,0:T(8,128)} %get-tuple-element.4) | data formatting | bytes 40960
  97.4 1.6 %copy.9 = f32[32,1280]{1,0:T(8,128)} copy(f32[32,1280]{1,0:T(8,128)} %get-tuple-element.5) | data formatting | bytes 327680
